TPU v7x, 256 devices: a whole 4x4x8 slice. The times are simulated.
256 devices in a mesh: expert: 8 (over y, core), shard: 32 (over x, z).
Axes of the slice: x: 4, y: 4, z: 8, core: 2. Of those that a mesh axis runs over, the one named last changes fastest.
Arguments:
- params: float32 [3, 8, 6144, 256], P(None, 'expert', 'shard'), may hold values from -3 to 3
- grads: float32 [3, 8, 6144, 256], P(None, 'expert', 'shard')
- moment: float32 [3, 8, 6144, 256], P(None, 'expert', 'shard'), may hold values from -0.6 to 0.6
- second: float32 [3, 8, 64], P(None, 'expert'), may hold values from 0.002 to 0.2
- step: int32 [1], replicated, may hold values from 1 to 8
- block_map: int32 [256], replicated, may hold values from 0 to 63, never falling along the last dimension, each value on 1 to 8 neighbouring positions
Outputs:
- new_weights: bfloat16 [3, 8, 6144, 256], P(None, 'expert')
- new_moment: float32 [3, 8, 6144, 256], P(None, 'expert', 'shard')
- new_second: float32 [3, 8, 64], P(None, 'expert')
Inputs may be any that keep to these rules, and one draw needn't show every extreme that they name: `block_map`: every block holds at least one neuron and at most 8.
All inputs are finite; a program needn't handle non-finite values.
Results may differ from a plain program's by a relative error of at most 0.001.
Values may be sent and summed in bfloat16 or wider, within the bound.
No kernel may reach another device: no remote copies, remote signals or barrier semaphores. Data moves between devices by JAX's collectives and lax.ppermute only.
A program may use at most 64 MiB of HBM per device.

v0:
```python
import math
import jax
import jax.numpy as jnp
from jax import lax
from jax.sharding import PartitionSpec as P

LEARN_RATE = 0.05
DECAY_WEIGHT = 0.1
BETA_FIRST = 0.9
BETA_SECOND = 0.95
epsilon = 1e-08


def copy_for_each(x, axis):
    length = lax.axis_size(axis)
    return lax.all_to_all(jnp.broadcast_to(x[None], (length, *x.shape)), axis, 0, 0, tiled=True)


def taken_together(x, axis):
    everything = copy_for_each(x, axis)
    return jnp.sum(everything, axis=0)


def body(params, grads, moment, second, step, block_map):
    blocks = second.shape[2]
    member_table = (block_map[:, None] == jnp.arange(blocks, dtype=jnp.int32)[None, :]).astype(
        jnp.float32
    )
    members = jnp.sum(member_table, axis=0)
    width = grads.shape[2] * lax.axis_size("shard")
    squares = jnp.sum(grads * grads, axis=2)
    local_sums = jnp.einsum("ken,nb->keb", squares, member_table, precision=lax.Precision.HIGHEST)
    block_sums = taken_together(local_sums, "shard")
    total = taken_together(jnp.sum(block_sums), "expert")
    limit = math.sqrt(3 * lax.axis_size("expert") * grads.shape[1] * width * grads.shape[3])
    clip = jnp.minimum(1.0, limit / (jnp.sqrt(total) + 1e-06))
    new_second = BETA_SECOND * second + (1.0 - BETA_SECOND) * clip * clip * block_sums / (
        width * members
    )
    new_moment = BETA_FIRST * moment + (1.0 - BETA_FIRST) * clip * grads
    step_value = step[0].astype(jnp.float32)
    first_fix = 1.0 - jnp.power(jnp.float32(BETA_FIRST), step_value)
    second_fix = 1.0 - jnp.power(jnp.float32(BETA_SECOND), step_value)
    divisor = jnp.sqrt(new_second / second_fix) + epsilon
    by_neuron = jnp.einsum("keb,nb->ken", divisor, member_table, precision=lax.Precision.HIGHEST)
    updated = (
        params * (1.0 - LEARN_RATE * DECAY_WEIGHT)
        - LEARN_RATE * (new_moment / first_fix) / by_neuron[:, :, None, :]
    )
    new_weights = lax.all_gather(updated.astype(jnp.bfloat16), "shard", axis=2, tiled=True)
    return (new_weights, new_moment, new_second)


def solution(mesh):
    placed = (
        P(None, "expert", "shard", None),
        P(None, "expert", "shard", None),
        P(None, "expert", "shard", None),
        P(None, "expert", None),
        P(),
        P(),
    )
    return jax.shard_map(
        body,
        mesh=mesh,
        in_specs=placed,
        out_specs=(
            P(None, "expert", None, None),
            P(None, "expert", "shard", None),
            P(None, "expert", None),
        ),
        check_vma=False,
    )
```

profile of v0, /device:TPU:1, one launch (start us, length us, event | category | flops | bytes accessed | tf_op | source)
XLA Modules:
  0.0 160.5 jit_solution(13806636719966661453)
XLA Ops:
  7.2 1.1 multiply_reduce_fusion
  8.3 0.8 fusion.1
  9.1 0.1 broadcast_in_dim.4
  9.2 0.5 broadcast.38
  9.7 0.8 reduce.4
  10.5 0.7 reshape.75
  11.2 11.9 %all-to-all-start = ((f32[32,1,192]{2,1,0:T(1,128)}), f32[32,1,192]{2,1,0:T(1,128)S(1)}, u32[]{:S(2)}, u32[]{:S(2)}) async-start(f32[32,1,192]{2,1,0:T(1,128)} %reshape.75), calls=%async_computation | async-start | bytes 65536 | tf_op jit(solution)/shard_map/all_to_all | solution.py:16
  23.0 0.0 all-gather.2.cloned.1.call-start
  23.1 0.8 convert_reduce_fusion
  24.6 7.2 %all-to-all-done = f32[32,1,192]{2,1,0:T(1,128)S(1)} async-done(((f32[32,1,192]{2,1,0:T(1,128)}), f32[32,1,192]{2,1,0:T(1,128)S(1)}, u32[]{:S(2)}, u32[]{:S(2)}) %all-to-all-start) | async-done | bytes 24608 | tf_op jit(solution)/shard_map/all_to_all | solution.py:16
  31.8 0.7 reduce.5
  32.5 0.1 reshape.76
  32.6 0.7 fusion.11
  33.3 0.6 broadcast_in_dim.5
  34.0 11.0 %all_to_all.11 = f32[8,1,1]{2,1,0:T(1,128)S(1)} all-to-all(f32[8,1,1]{2,1,0:T(1,128)S(1)} %broadcast_in_dim.5), channel_id=1, replica_groups=mesh['expert'=8,'shard'=32] {'expert'}, dimensions={0} | all-to-all | bytes 64 | tf_op jit(solution)/shard_map/all_to_all | solution.py:16
  45.0 0.6 reduce_sum.47
  46.3 0.7 divide_add_fusion
  47.0 0.8 fusion
  47.8 2.5 %subtract_convert_fusion = (bf16[3,1,192,256]{3,2,1,0:T(8,128)(2,1)}, f32[3,1,192,256]{3,2,1,0:T(8,128)}) fusion(f32[3,1,192,256]{3,2,1,0:T(8,128)} %param.6, f32[3,256]{1,0:T(4,128)S(1)} %fusion, f32[]{:T(128)} %bitcast, f32[3,1,192,256]{3,2,1,0:T(8,128)} %param.7, f32[]{:T(128)S(6)} %mul_shard_map.3, f32[3,1,192,256]{3,2,1,0:T(8,128)} %param.8), kind=kLoop, calls=%fused_computation | loop fusion | flops 1327104 | bytes 2657288 | tf_op jit(solution)/shard_map/convert_element_type | solution.py:50
  50.3 0.0 all-gather.2.cloned.1.call-update
  50.3 0.6 copy.15
  50.9 94.7 %all-gather.2.cloned.1.call-done = bf16[3,1,6144,256]{3,2,1,0:T(8,128)(2,1)} async-done(((bf16[3,1,192,256]{3,2,1,0:T(8,128)(2,1)}), bf16[3,1,6144,256]{3,2,1,0:T(8,128)(2,1)}) %all-gather.2.cloned.1.call-update) | async-done | bytes 9437200 | tf_op jit(solution)/shard_map/all_gather | solution.py:50
  145.6 8.0 %copy.24 = bf16[3,1,6144,256]{3,2,1,0:T(8,128)(2,1)} copy(bf16[3,1,6144,256]{3,2,1,0:T(8,128)(2,1)} %all-gather.2.cloned.1.call-done) | data formatting | bytes 18874368
  (1 shorter events, 0.0 us)
Async XLA Ops:
  11.2 20.6 %all-to-all-start = ((f32[32,1,192]{2,1,0:T(1,128)}), f32[32,1,192]{2,1,0:T(1,128)S(1)}, u32[]{:S(2)}, u32[]{:S(2)}) async-start(f32[32,1,192]{2,1,0:T(1,128)} %reshape.75), calls=%async_computation | async-start | bytes 65536 | tf_op jit(solution)/shard_map/all_to_all | solution.py:16
  23.0 122.6 %all-gather.2.cloned.1.call-start = ((), (), s32[]{:S(2)}) async-start(), calls=%async_computation.2 | async-start | bytes 9732096 | tf_op jit(solution)/shard_map/all_gather | solution.py:50
Sparse Core Ops, SparseCore 0:
  50.5 95.1 all-gather.1
where the time goes:
time: 161 us; the launch traced here: 160 us
  waiting for transfers between devices  102 us (63%)
  between operations  15.6 us (10%)
  starting transfers between devices  11.9 us (7%)
  blocking collectives  11 us (7%)
  local copies, waits for them, and re-layouts  10.6 us (7%)
  other arithmetic  7.94 us (5%)
  matrix products  1.61 us (1%)
    all_gather x1, waiting for transfers between devices, body(): lax.all_gather(updated.astype(jnp.bfloat16), 'shard', axis=2, tiled=True)  94.7 us
    all_to_all x1, starting transfers between devices, copy_for_each(): lax.all_to_all(jnp.broadcast_to(x[None], (length, *x.shape)), axis, 0, 0,...  11.9 us
    all_to_all x1, blocking collectives, copy_for_each(): lax.all_to_all(jnp.broadcast_to(x[None], (length, *x.shape)), axis, 0, 0,...  11 us
    unnamed x4, local copies, waits for them, and re-layouts  9.39 us
    all_to_all x1, waiting for transfers between devices, copy_for_each(): lax.all_to_all(jnp.broadcast_to(x[None], (length, *x.shape)), axis, 0, 0,...  7.18 us
  transfers between devices with their start and end apart: 2, of which 2 were waited for; matrix products, arithmetic and copies ran while one was open for 1% of the time, Pallas kernels for 0%

commit v1 on v0

--- a/solution.py
+++ b/solution.py
@@ -9,6 +9,11 @@
 BETA_FIRST = 0.9
 BETA_SECOND = 0.95
 epsilon = 1e-08
+
+
+def quarters_place(z_in):
+    mixed_arr = jnp.concatenate([z_in] * lax.axis_size("shard"), axis=2)
+    return lax.all_to_all(mixed_arr, "shard", 2, 2, tiled=True)
 
 
 def copy_for_each(x, axis):
@@ -47,7 +52,7 @@
         params * (1.0 - LEARN_RATE * DECAY_WEIGHT)
         - LEARN_RATE * (new_moment / first_fix) / by_neuron[:, :, None, :]
     )
-    new_weights = lax.all_gather(updated.astype(jnp.bfloat16), "shard", axis=2, tiled=True)
+    new_weights = quarters_place(updated.astype(jnp.bfloat16))
     return (new_weights, new_moment, new_second)
 
 

time: 161 us -> 409 us (2.54)
  the two profiles are of different devices: /device:TPU:1 before, /device:TPU:167 now
where the time goes in v1:
time: 409 us
  waiting for transfers between devices  305 us (75%)
  local copies, waits for them, and re-layouts  62.4 us (15%)
  starting transfers between devices  19.3 us (5%)
  blocking collectives  10.7 us (3%)
  other arithmetic  7.84 us (2%)
    all_to_all x1, waiting for transfers between devices, quarters_place(): return lax.all_to_all(mixed_arr, 'shard', 2, 2, tiled=True)  303 us
    concatenate x2, local copies, waits for them, and re-layouts, quarters_place(): mixed_arr = jnp.concatenate([z_in] * lax.axis_size('shard'), axis=2)  49.5 us
    unnamed x34, local copies, waits for them, and re-layouts  11.6 us
    all_to_all x1, blocking collectives, copy_for_each(): lax.all_to_all(jnp.broadcast_to(x[None], (length, *x.shape)), axis, 0, 0,...  10.7 us
    all_to_all x1, starting transfers between devices, quarters_place(): return lax.all_to_all(mixed_arr, 'shard', 2, 2, tiled=True)  10.5 us
    all_to_all x1, starting transfers between devices, copy_for_each(): lax.all_to_all(jnp.broadcast_to(x[None], (length, *x.shape)), axis, 0, 0,...  8.8 us
  transfers between devices with their start and end apart: 2, of which 2 were waited for; matrix products, arithmetic and copies ran while one was open for 0% of the time, Pallas kernels for 0%

profile of v1, /device:TPU:167, one launch (start us, length us, event | category | flops | bytes accessed | tf_op | source)
XLA Modules:
  0.0 408.8 jit_solution(12837783588795937898)
XLA Ops:
  0.6 1.1 multiply_reduce_fusion
  1.8 0.8 fusion.1
  2.6 0.1 broadcast_in_dim.4
  2.6 0.5 broadcast.38
  3.1 0.8 reduce.4
  3.9 0.7 reshape.75
  4.6 8.8 %all-to-all-start = ((f32[32,1,192]{2,1,0:T(1,128)}), f32[32,1,192]{2,1,0:T(1,128)S(1)}, u32[]{:S(2)}, u32[]{:S(2)}) async-start(f32[32,1,192]{2,1,0:T(1,128)} %reshape.75), calls=%async_computation | async-start | bytes 65536 | tf_op jit(solution)/shard_map/all_to_all | solution.py:21
  13.4 0.8 convert_reduce_fusion
  15.0 2.0 all-to-all-done
  17.0 0.7 reduce.5
  17.7 0.1 reshape.76
  17.8 0.7 fusion.11
  18.5 0.6 broadcast_in_dim.5
  19.1 10.7 %all_to_all.16 = f32[8,1,1]{2,1,0:T(1,128)S(1)} all-to-all(f32[8,1,1]{2,1,0:T(1,128)S(1)} %broadcast_in_dim.5), channel_id=1, replica_groups=mesh['expert'=8,'shard'=32] {'expert'}, dimensions={0} | all-to-all | bytes 64 | tf_op jit(solution)/shard_map/all_to_all | solution.py:21
  29.9 0.6 reduce_sum.47
  31.2 0.7 divide_add_fusion
  31.9 0.8 fusion
  32.7 2.4 constant_dynamic-update-slice_fusion.31
  36.0 49.5 %copy.27 = bf16[3,1,6144,256]{3,0,1,2:T(4,128)(2,1)} copy(bf16[3,1,6144,256]{3,2,1,0:T(8,128)(2,1)S(1)} %constant_dynamic-update-slice_fusion) | data formatting | bytes 18874368 | tf_op jit(solution)/shard_map/concatenate | solution.py:15
  85.5 10.5 %all-to-all-start.2 = ((bf16[3,1,6144,256]{3,0,1,2:T(4,128)(2,1)}), bf16[3,1,6144,256]{3,0,1,2:T(4,128)(2,1)}, u32[]{:S(2)}, u32[]{:S(2)}) async-start(bf16[3,1,6144,256]{3,0,1,2:T(4,128)(2,1)} %copy.27), calls=%async_computation.2 | async-start | bytes 25165824 | tf_op jit(solution)/shard_map/all_to_all | solution.py:16
  96.0 0.6 copy.29
  96.6 302.6 %all-to-all-done.2 = bf16[3,1,6144,256]{3,0,1,2:T(4,128)(2,1)} async-done(((bf16[3,1,6144,256]{3,0,1,2:T(4,128)(2,1)}), bf16[3,1,6144,256]{3,0,1,2:T(4,128)(2,1)}, u32[]{:S(2)}, u32[]{:S(2)}) %all-to-all-start.2) | async-done | bytes 9437216 | tf_op jit(solution)/shard_map/all_to_all | solution.py:16
  399.1 9.6 %copy.28 = bf16[3,1,6144,256]{3,2,1,0:T(8,128)(2,1)} copy(bf16[3,1,6144,256]{3,0,1,2:T(4,128)(2,1)} %all-to-all-done.2) | data formatting | bytes 18874368
  (32 shorter events, 0.7 us)
Async XLA Ops:
  4.6 12.3 %all-to-all-start = ((f32[32,1,192]{2,1,0:T(1,128)}), f32[32,1,192]{2,1,0:T(1,128)S(1)}, u32[]{:S(2)}, u32[]{:S(2)}) async-start(f32[32,1,192]{2,1,0:T(1,128)} %reshape.75), calls=%async_computation | async-start | bytes 65536 | tf_op jit(solution)/shard_map/all_to_all | solution.py:21
  85.5 313.6 %all-to-all-start.2 = ((bf16[3,1,6144,256]{3,0,1,2:T(4,128)(2,1)}), bf16[3,1,6144,256]{3,0,1,2:T(4,128)(2,1)}, u32[]{:S(2)}, u32[]{:S(2)}) async-start(bf16[3,1,6144,256]{3,0,1,2:T(4,128)(2,1)} %copy.27), calls=%async_computation.2 | async-start | bytes 25165824 | tf_op jit(solution)/shard_map/all_to_all | solution.py:16
